TPU v7x, 32 devices: a whole 2x2x4 slice. The times are simulated.
32 devices in a mesh: box: 16 (over z, y, core), lev: 2 (over x).
Axes of the slice: x: 2, y: 2, z: 4, core: 2. Of those that a mesh axis runs over, the one named last changes fastest.
Arguments:
- fine: float32 [96, 5, 32, 1024], P(('box', 'lev')), may hold values from -12 to 12
- coarse: float32 [5, 256, 32, 128], P(None, 'box', 'lev'), may hold values from -6 to 6
- owner_map: int32 [96, 2], P(('box', 'lev')), may hold values from -2 to 7, as said below
- patch_count: int32 [32], P(('box', 'lev')), may hold values from 1 to 3, as said below
- face_mask: int32 [96, 6], P(('box', 'lev')), may hold values 0 or 1
Outputs:
- updated: float32 [5, 256, 32, 128], P(None, 'box', 'lev')
- ghost: float32 [96, 6, 5, 2048], P(('box', 'lev'))
Inputs may be any that keep to these rules, and one draw needn't show every extreme that they name: `owner_map`: row p is fine patch p of device j = p // 3: column 0 is the offset k of its coarse owner, device (j + k) mod 32, one of -2, -1, 1, 2 and different for the 3 rows of one device; column 1 is a region r of that owner's block, 0 to 7. Rows of patches that are not live carry entries of the same kind and are ignored. No two live patches name the same owner and region. Device j holds live patches j * 3 to j * 3 + patch_count[j] - 1. Some device holds 3 live patches.
All inputs are finite; a program needn't handle non-finite values. No bound on the sum of `face_mask` on one device may be relied on, other than what follows from the above.
Results may differ from a plain program's by a relative error of at most 0.0003.
Values sent between devices are 32-bit elements; how exact they have to be, the bound alone decides.
A program may use at most 128 MiB of HBM per device.

v0:
```python
import functools

import jax
import jax.numpy as jnp
from jax import lax
from jax.experimental import pallas as pl
from jax.experimental.pallas import tpu as pltpu
from jax.sharding import PartitionSpec as P

DELTAS = (-2, -1, 1, 2)
LANES = 128
SUB = 8
F32 = jnp.float32
BF16 = jnp.bfloat16
MESH_ID = pl.DeviceIdType.MESH


def iota(shape, dim):
    return lax.broadcasted_iota(jnp.int32, shape, dim)


def split(values):
    high = values.astype(BF16)
    return high, (values - high.astype(F32)).astype(BF16)


def split_lanes(values):
    return jnp.concatenate(split(values), axis=1)


def times_transposed(left, right):
    return lax.dot_general(left, right, (((1,), (1,)), ((), ())), preferred_element_type=F32)


def both(table):
    return jnp.concatenate([table, table], axis=0)


def kernel(
    n_box, n_lev, slots, fields, edge,
    owner, count, mask, fine, coarse, updated, ghost,
    half_a, half_b, send1, recv1, halo_out, halo_in, corner_out, corner_in,
    planes, zrows, send3, recv3, place_table,
    s1, r1, s2, r2, s3, r3,
):
    fine_edge = 2 * edge
    block = fields * edge
    ext = edge + SUB
    z_at = 4 * ext
    d_at = 8 * ext
    c_at = d_at + 4 * edge
    rows3 = c_at + edge
    n_dev = n_box * n_lev
    box = lax.axis_index("box")
    lev = lax.axis_index("lev")
    me = box * n_lev + lev

    def shifted(by):
        other = lax.rem(me + (by + n_dev), n_dev)
        return (lax.div(other, n_lev), lax.rem(other, n_lev))

    def beside(dx, dy):
        return (lax.rem(box + (dx + n_box), n_box), lax.rem(lev + (dy + n_lev), n_lev))

    sides = (beside(-1, 0), beside(1, 0), beside(0, -1), beside(0, 1))
    corners = tuple(beside(2 * cx - 1, 2 * cy - 1) for cx in (0, 1) for cy in (0, 1))
    barrier = pltpu.get_barrier_semaphore()
    peers = [shifted(delta) for delta in DELTAS] + list(sides) + list(corners)
    for peer in peers:
        pl.semaphore_signal(barrier, inc=1, device_id=peer, device_id_type=MESH_ID)

    live_count = count[0]
    chosen = [
        [(s < live_count) & (owner[s, 0] == delta) for delta in DELTAS] for s in range(slots)
    ]
    weight = [[jnp.where(c, 1.0, 0.0).astype(F32) for c in row] for row in chosen]

    q = iota((fine_edge * fine_edge, edge * edge), 0)
    c = iota((fine_edge * fine_edge, edge * edge), 1)
    goal = (q // (2 * fine_edge)) * edge + (q % fine_edge) // 2
    table = jnp.where(goal == c, 0.125, 0.0).astype(BF16)
    frows = fields * fine_edge
    for s in range(slots):
        high, low = split(fine[s * frows:(s + 1) * frows, :])
        got = jnp.dot(high, table, preferred_element_type=F32) + jnp.dot(
            low, table, preferred_element_type=F32
        )
        half_a[s * frows:(s + 1) * frows, :] = got[:, :LANES]
        half_b[s * frows:(s + 1) * frows, :] = got[:, LANES:]
    for h, half in enumerate((half_a, half_b)):
        averaged = [
            half[pl.ds(s * frows, block, stride=2), :] + half[pl.ds(s * frows + 1, block, stride=2), :]
            for s in range(slots)
        ]
        for k in range(4):
            total = averaged[0] * weight[0][k]
            for s in range(1, slots):
                total = total + averaged[s] * weight[s][k]
            send1[k, 0:block, h * LANES:(h + 1) * LANES] = total
    for k in range(4):
        region = jnp.int32(-1)
        for s in range(slots):
            region = jnp.where(chosen[s][k], owner[s, 1], region)
        send1[k, block:block + SUB, :] = jnp.full((SUB, 2 * LANES), 1.0, F32) * region.astype(F32)

    pl.semaphore_wait(barrier, len(peers))
    first = []
    for k, delta in enumerate(DELTAS):
        copy = pltpu.make_async_remote_copy(
            src_ref=send1.at[k], dst_ref=recv1.at[k], send_sem=s1.at[k], recv_sem=r1.at[k],
            device_id=shifted(delta), device_id_type=MESH_ID,
        )
        copy.start()
        first.append(copy)

    for pair in range(4):
        row = iota((LANES, 2 * LANES), 0)
        col = iota((LANES, 2 * LANES), 1)
        hit = (row // edge == 2 * pair + col // LANES) & (row % edge == col % edge)
        place_table[pair] = both(jnp.where(hit, 1.0, 0.0).astype(BF16))
    planes[...] = jnp.zeros_like(planes)
    zrows[...] = jnp.zeros_like(zrows)
    corner_out[...] = jnp.zeros_like(corner_out)
    for k in range(4):
        send3[k * rows3 + z_at:k * rows3 + d_at, :] = jnp.zeros((4 * ext, LANES), F32)

    for copy in first:
        copy.wait_recv()

    group = (iota((1, LANES), 1) // edge).astype(F32)
    region_rows = [recv1[k, block:block + 1, 0:LANES] for k in range(4)]
    here = [group == region_rows[k] for k in range(4)]
    for h in range(2):
        stacked = split_lanes(
            jnp.concatenate([recv1[k, 0:block, h * LANES:(h + 1) * LANES] for k in range(4)], axis=0)
        )
        for pair in range(4):
            spread = jnp.dot(stacked, place_table[pair], preferred_element_type=F32)
            for odd in range(2):
                y = h * SUB + 2 * pair + odd
                merged = coarse[pl.ds(y, block, stride=edge), :]
                for k in range(4):
                    merged = jnp.where(
                        here[k], spread[k * block:(k + 1) * block, odd * LANES:(odd + 1) * LANES], merged
                    )
                updated[pl.ds(y, block, stride=edge), :] = merged
                if y < 2:
                    halo_out[2, y * block:(y + 1) * block, :] = merged
                if y >= edge - 2:
                    layer = edge - 1 - y
                    halo_out[3, layer * block:(layer + 1) * block, :] = merged
    for f in range(fields):
        for layer in range(2):
            for side, x in ((0, layer), (1, edge - 1 - layer)):
                at = f * edge * edge + x * edge
                to = (layer * fields + f) * edge
                halo_out[side, to:to + edge, :] = updated[at:at + edge, :]
    for cx in (0, 1):
        for cy in (0, 1):
            for f in range(fields):
                at = f * edge * edge + cx * (edge - 1) * edge + cy * (edge - 1)
                corner_out[2 * cx + cy, f:f + 1, :] = updated[at:at + 1, :]

    second = []
    for side in range(4):
        copy = pltpu.make_async_remote_copy(
            src_ref=halo_out.at[side], dst_ref=halo_in.at[side ^ 1],
            send_sem=s2.at[side], recv_sem=r2.at[side ^ 1],
            device_id=sides[side], device_id_type=MESH_ID,
        )
        copy.start()
        second.append(copy)
    for corner in range(4):
        copy = pltpu.make_async_remote_copy(
            src_ref=corner_out.at[corner], dst_ref=corner_in.at[3 - corner],
            send_sem=s2.at[4 + corner], recv_sem=r2.at[4 + 3 - corner],
            device_id=corners[corner], device_id_type=MESH_ID,
        )
        copy.start()
        second.append(copy)

    lane = iota((1, LANES), 1).astype(F32)

    def pick(k, place):
        t = lane - edge * region_rows[k] - place
        return jnp.where((t == 0.0) | (t == LANES) | (t == -LANES), 1.0, 0.0)

    i_side = iota((ext, 1), 0)
    place = jnp.where(i_side == edge, -1, jnp.where(i_side == edge + 1, edge, i_side)).astype(F32)
    used = i_side < edge + 2
    side_table = jnp.concatenate(
        [jnp.where(used, pick(k, place), 0.0) for k in range(4)], axis=0
    ).astype(BF16)
    side_table = jnp.concatenate([side_table, side_table], axis=1)
    i_z = iota((SUB, 1), 0)
    plus = jnp.where(i_z == 0, -1, jnp.where(i_z == 1, 0, jnp.where(i_z == 2, edge, edge + 1)))
    minus = jnp.where(i_z == 1, -2, edge - 1)
    z_list = []
    for k in range(4):
        up = pick(k, plus.astype(F32))
        down = jnp.where((i_z == 1) | (i_z == 3), pick(k, minus.astype(F32)), 0.0)
        z_list.append(jnp.where(i_z < 4, up - down, 0.0))
    z_table = jnp.concatenate(z_list, axis=0).astype(BF16)
    z_table = jnp.concatenate([z_table, z_table], axis=1)

    def z_store(v, values):
        for k in range(4):
            send3[pl.ds(k * rows3 + z_at + v, 4, stride=ext), :] = values[k * SUB:k * SUB + 4, :]

    for v in range(edge):
        for f in range(fields):
            zrows[pl.ds(v * LANES + f, edge, stride=SUB), :] = updated[
                pl.ds(f * edge * edge + v, edge, stride=edge), :
            ]
    for v in range(0, edge, 2):
        got = times_transposed(z_table, split_lanes(zrows[v * LANES:(v + 2) * LANES, :]))
        z_store(v, got[:, :LANES])
        z_store(v + 1, got[:, LANES:])

    def line_tables(cell, odd):
        i = iota((ext, LANES), 0)
        at = jnp.where(i == edge, -1, jnp.where(i == edge + 1, edge, i))
        at = jnp.where(i < edge + 2, at, -9)
        plain = jnp.where(at == cell, 1.0, 0.0)
        sign = jnp.where(odd, 0.125, -0.125)
        slope = jnp.where(at == cell + 1, sign, jnp.where(at == cell - 1, -sign, 0.0))
        full = both(jnp.concatenate([plain, plain + slope], axis=1)).astype(BF16)
        return full, both((plain[:edge] * 0.125)).astype(BF16)

    l2 = iota((ext, LANES), 1)
    w_table, w_diff = line_tables((l2 % fine_edge) // 2, l2 % 2 == 1)
    v_table, v_diff = line_tables((l2 % (2 * fine_edge)) // 4, (l2 // 2) % 2 == 1)
    row = iota((LANES, LANES), 0)
    col = iota((LANES, LANES), 1)
    line_v = both(jnp.where(row // SUB == (col % (2 * fine_edge)) // 4, 1.0, 0.0).astype(BF16))

    for copy in second:
        copy.wait_recv()

    for side in range(4):
        near = 1.0 if side % 2 == 0 else -1.0
        for f in range(fields):
            a = f * edge
            adjacent = halo_in[side, a:a + edge, :]
            far = halo_in[side, block + a:block + a + edge, :]
            own = halo_out[side, a:a + edge, :]
            planes[pl.ds(2 * side * LANES + f, edge, stride=SUB), :] = adjacent
            planes[pl.ds((2 * side + 1) * LANES + f, edge, stride=SUB), :] = (own - far) * near
    for corner in range(4):
        planes[8 * LANES + corner * SUB:8 * LANES + (corner + 1) * SUB, :] = corner_in[corner]
    for side in range(4):
        both_planes = split_lanes(planes[2 * side * LANES:(2 * side + 2) * LANES, :])
        got = times_transposed(side_table, both_planes)
        for k in range(4):
            at = k * rows3
            send3[at + side * ext:at + (side + 1) * ext, :] = got[k * ext:(k + 1) * ext, :LANES]
            to = at + d_at + side * edge
            send3[to:to + edge, :] = got[k * ext:k * ext + edge, LANES:]
        if side >= 2:
            z_store(edge + side - 2, times_transposed(z_table, both_planes[:LANES, :]))
    got = times_transposed(side_table, split_lanes(planes[8 * LANES:9 * LANES, :]))
    for k in range(4):
        send3[k * rows3 + c_at:k * rows3 + c_at + edge, :] = got[k * ext:k * ext + edge, :]

    third = []
    for k, delta in enumerate(DELTAS):
        copy = pltpu.make_async_remote_copy(
            src_ref=send3.at[pl.ds(k * rows3, rows3)], dst_ref=recv3.at[k],
            send_sem=s3.at[k], recv_sem=r3.at[k],
            device_id=shifted(-delta), device_id_type=MESH_ID,
        )
        copy.start()
        third.append(copy)
    for copy in third:
        copy.wait_recv()

    lanes8 = iota((SUB, LANES), 1)
    low_half = lanes8 < 2 * fine_edge
    half_sign = jnp.where(low_half, -0.125, 0.125)
    quarter = (lanes8 // fine_edge) % 2 == 1
    quarter_slope = jnp.where(quarter, 0.125, -0.125)
    quarter_sign = jnp.where(quarter, 1.0, -1.0)
    last_sign = jnp.where(lanes8 % 2 == 1, 1.0, -1.0)
    own_field = lanes8 % SUB == iota((SUB, LANES), 0)

    def spread_plane(s, at, length, table):
        total = recv3[0, at:at + length, :] * weight[s][0]
        for k in range(1, 4):
            total = total + recv3[k, at:at + length, :] * weight[s][k]
        high = total.astype(BF16).astype(F32)
        tall = jnp.concatenate([high, total - high], axis=0)
        return total, jnp.dot(tall.T.astype(BF16), table, preferred_element_type=F32)

    def cut(values, m):
        return values[m * SUB:(m + 1) * SUB, :]

    for s in range(slots):
        keep = [
            jnp.where((s < live_count) & (mask[s, face] > 0), 1.0, 0.0).astype(F32)
            for face in range(6)
        ]
        _, lines = spread_plane(s, c_at, edge, w_diff)
        line = [cut(lines, corner) * 8.0 for corner in range(4)]
        edges = []
        for side in range(4):
            raw, centre = spread_plane(s, side * ext, ext, w_table)
            _, diff = spread_plane(s, d_at + side * edge, edge, w_diff)
            plain = [cut(centre, m)[:, :LANES] for m in range(edge)]
            full = [cut(centre, m)[:, LANES:] for m in range(edge)]
            high_side = side % 2
            if side < 2:
                edges.append(raw[edge:edge + 1, :])
                edges.append(raw[edge + 1:edge + 2, :])
                around = [line[2 * high_side]] + plain + [line[2 * high_side + 1]]
                for t in range(edge // 2):
                    base = jnp.where(low_half, full[2 * t], full[2 * t + 1])
                    slope = jnp.where(
                        low_half, around[2 * t + 2] - around[2 * t], around[2 * t + 3] - around[2 * t + 1]
                    )
                    across = jnp.where(low_half, cut(diff, 2 * t), cut(diff, 2 * t + 1))
                    base = base + slope * quarter_slope
                    at = t * LANES
                    ghost[s, side, :, at:at + LANES] = ((base - across) * keep[side])[:fields]
                    at = at + fine_edge * fine_edge
                    ghost[s, side, :, at:at + LANES] = ((base + across) * keep[side])[:fields]
            else:
                around = [line[high_side]] + plain + [line[2 + high_side]]
                for t in range(edge):
                    value = (
                        full[t] + (around[t + 2] - around[t]) * half_sign + cut(diff, t) * quarter_sign
                    )
                    ghost[s, side, :, t * LANES:(t + 1) * LANES] = (value * keep[side])[:fields]
        tall = jnp.concatenate([jnp.where(own_field, e, 0.0) for e in edges], axis=0)
        ends = jnp.dot(split_lanes(tall), line_v, preferred_element_type=F32)
        for z in range(2):
            _, centre = spread_plane(s, z_at + 2 * z * ext, ext, v_table)
            _, diff = spread_plane(s, z_at + (2 * z + 1) * ext, edge, v_diff)
            around = (
                [cut(ends, z)] + [cut(centre, m)[:, :LANES] for m in range(edge)] + [cut(ends, 2 + z)]
            )
            for t in range(edge):
                value = (
                    cut(centre, t)[:, LANES:]
                    + (around[t + 2] - around[t]) * half_sign
                    + cut(diff, t) * last_sign
                )
                ghost[s, 4 + z, :, t * LANES:(t + 1) * LANES] = (value * keep[4 + z])[:fields]

    for copy in first + second + third:
        copy.wait_send()


def body(n_box, n_lev, fine, coarse, owner_map, patch_count, face_mask):
    slots, fields, fine_edge, _ = fine.shape
    edge = fine_edge // 2
    block = fields * edge
    ext = edge + SUB
    rows3 = 8 * ext + 5 * edge
    vmem = pl.BlockSpec(memory_space=pltpu.VMEM)
    smem = pl.BlockSpec(memory_space=pltpu.SMEM)
    updated, ghost = pl.pallas_call(
        functools.partial(kernel, n_box, n_lev, slots, fields, edge),
        out_shape=(
            jax.ShapeDtypeStruct((block * edge, LANES), F32),
            jax.ShapeDtypeStruct((slots, 6, fields, 2 * fine_edge * fine_edge), F32),
        ),
        in_specs=[smem, smem, smem, vmem, vmem],
        out_specs=(vmem, vmem),
        scratch_shapes=[
            pltpu.VMEM((slots * fields * fine_edge, LANES), F32),
            pltpu.VMEM((slots * fields * fine_edge, LANES), F32),
            pltpu.VMEM((4, block + SUB, 2 * LANES), F32),
            pltpu.VMEM((4, block + SUB, 2 * LANES), F32),
            pltpu.VMEM((4, 2 * block, LANES), F32),
            pltpu.VMEM((4, 2 * block, LANES), F32),
            pltpu.VMEM((4, SUB, LANES), F32),
            pltpu.VMEM((4, SUB, LANES), F32),
            pltpu.VMEM((9 * LANES, LANES), F32),
            pltpu.VMEM((edge * LANES, LANES), F32),
            pltpu.VMEM((4 * rows3, LANES), F32),
            pltpu.VMEM((4, rows3, LANES), F32),
            pltpu.VMEM((4, 2 * LANES, 2 * LANES), BF16),
            pltpu.SemaphoreType.DMA((4,)),
            pltpu.SemaphoreType.DMA((4,)),
            pltpu.SemaphoreType.DMA((8,)),
            pltpu.SemaphoreType.DMA((8,)),
            pltpu.SemaphoreType.DMA((4,)),
            pltpu.SemaphoreType.DMA((4,)),
        ],
        compiler_params=pltpu.CompilerParams(collective_id=0, has_side_effects=True),
    )(
        owner_map, patch_count, face_mask,
        fine.reshape(slots * fields * fine_edge, fine_edge * fine_edge),
        coarse.reshape(block * edge, LANES),
    )
    return updated.reshape(coarse.shape), ghost


def solution(mesh):
    return jax.shard_map(
        functools.partial(body, mesh.shape["box"], mesh.shape["lev"]),
        mesh=mesh,
        in_specs=(
            P(("box", "lev"), None, None, None),
            P(None, "box", "lev", None),
            P(("box", "lev"), None),
            P(("box", "lev")),
            P(("box", "lev"), None),
        ),
        out_specs=(P(None, "box", "lev", None), P(("box", "lev"), None, None, None)),
        check_vma=False,
    )
```

profile of v0, /device:TPU:0, one launch (start us, length us, event | category | flops | bytes accessed | tf_op | source)
XLA Modules:
  0.0 35.5 jit_solution(2516834512235662917)
XLA Ops:
  1.3 1.3 %copy.7.owner = s32[3,2]{1,0:T(4,128)} copy(s32[3,2]{0,1:T(2,128)} %param.7) | data formatting | bytes 48 | tf_op args[2]
  2.6 29.3 %shard_map.68 = (f32[1280,128]{1,0:T(8,128)}, f32[3,6,5,2048]{3,2,1,0:T(8,128)}) custom-call(s32[3,2]{1,0:T(4,128)} %copy.7.owner, s32[1]{0:T(128)S(6)} %copy.10.count, s32[3,6]{1,0:T(4,128)} %mask.1, f32[480,1024]{1,0:T(8,128)} %bitcast.3, f32[1280,128]{1,0:T(8,128)} %bitcast.5), custom_call_target="tpu_custom_call" | custom-call | tf_op jit(solution)/shard_map/pallas_call | solution.py:361
  31.9 0.0 copy-start
  31.9 2.7 %copy.8 = f32[3,6,5,2048]{3,1,2,0:T(8,128)} copy(f32[3,6,5,2048]{3,2,1,0:T(8,128)} %get-tuple-element.7) | data formatting | bytes 1474560
  34.6 0.0 copy-done
  34.6 0.8 %copy.11 = f32[5,16,16,128]{3,2,1,0:T(8,128)} copy(f32[5,16,16,128]{3,2,1,0:T(8,128)S(1)} %bitcast.4) | data formatting | bytes 1310720
Async XLA Ops:
  31.9 2.7 %copy-start = (f32[1280,128]{1,0:T(8,128)S(1)}, f32[1280,128]{1,0:T(8,128)}, u32[]{:S(2)}) copy-start(f32[1280,128]{1,0:T(8,128)} %get-tuple-element.4) | copy-start | bytes 1966084
where the time goes:
time: 35.7 us; the launch traced here: 35.5 us
  Pallas kernels  29.3 us (82%)
  local copies, waits for them, and re-layouts  4.89 us (14%)
  between operations  1.29 us (4%)
    pallas_call x1, Pallas kernels, body(): pl.pallas_call(functools.partial(kernel, n_box, n_lev, slots, fields, edg...  29.3 us
    unnamed x5, local copies, waits for them, and re-layouts  4.89 us

commit v1 on v0

v1 whole, which is shorter than its diff:
```python
import functools

import jax
import jax.numpy as jnp
from jax import lax
from jax.experimental import pallas as pl
from jax.experimental.pallas import tpu as pltpu
from jax.sharding import PartitionSpec as P

DELTAS = (-2, -1, 1, 2)
LANES = 128
SUB = 8
F32 = jnp.float32
BF16 = jnp.bfloat16
MESH_ID = pl.DeviceIdType.MESH


def iota(shape, dim):
    return lax.broadcasted_iota(jnp.int32, shape, dim)


def split(values):
    high = values.astype(BF16)
    return high, (values - high.astype(F32)).astype(BF16)


def split_lanes(values):
    return jnp.concatenate(split(values), axis=1)


def times_transposed(left, right):
    return lax.dot_general(left, right, (((1,), (1,)), ((), ())), preferred_element_type=F32)


def both(table):
    return jnp.concatenate([table, table], axis=0)


def window_rows(edge):
    z_at = 4 * edge
    d_at = 6 * edge
    return 14 * edge, z_at, d_at, d_at + 4 * edge, d_at + 6 * edge, d_at + 7 * edge


def kernel(
    n_box, n_lev, slots, fields, edge,
    owner, count, fine_far, coarse_far, updated, window,
    fine, coarse, half_a, half_b, send1, recv1, halo_out, halo_in, corner_out, corner_in,
    planes, zrows, send3, recv3, place_table,
    load, s1, r1, s2, r2, s3, r3,
):
    fine_edge = 2 * edge
    block = fields * edge
    ext = edge + SUB
    rows3, z_at, d_at, zd_at, c_at, e_at = window_rows(edge)
    frows = fields * fine_edge
    cut = (fields + 1) // 2
    chunks = ((0, cut), (cut, fields))
    loads = {}
    for part, (f0, f1) in enumerate(chunks):
        for s in range(slots):
            rows = pl.ds(s * frows + f0 * fine_edge, (f1 - f0) * fine_edge)
            loads[part, s] = pltpu.make_async_copy(
                fine_far.at[rows], fine.at[rows], load.at[part * slots + s]
            )
            loads[part, s].start()
    coarse_load = pltpu.make_async_copy(coarse_far, coarse, load.at[2 * slots])
    coarse_load.start()
    n_dev = n_box * n_lev
    box = lax.axis_index("box")
    lev = lax.axis_index("lev")
    me = box * n_lev + lev

    def shifted(by):
        other = lax.rem(me + (by + n_dev), n_dev)
        return (lax.div(other, n_lev), lax.rem(other, n_lev))

    def beside(dx, dy):
        return (lax.rem(box + (dx + n_box), n_box), lax.rem(lev + (dy + n_lev), n_lev))

    sides = (beside(-1, 0), beside(1, 0), beside(0, -1), beside(0, 1))
    corners = tuple(beside(2 * cx - 1, 2 * cy - 1) for cx in (0, 1) for cy in (0, 1))
    barrier = pltpu.get_barrier_semaphore()
    peers = [shifted(delta) for delta in DELTAS] + list(sides) + list(corners)
    for peer in peers:
        pl.semaphore_signal(barrier, inc=1, device_id=peer, device_id_type=MESH_ID)

    live_count = count[0]
    chosen = [
        [(s < live_count) & (owner[0, s] == delta) for delta in DELTAS] for s in range(slots)
    ]
    weight = [[jnp.where(c, 1.0, 0.0).astype(F32) for c in row] for row in chosen]

    q = iota((fine_edge * fine_edge, edge * edge), 0)
    c = iota((fine_edge * fine_edge, edge * edge), 1)
    goal = (q // (2 * fine_edge)) * edge + (q % fine_edge) // 2
    table = jnp.where(goal == c, 0.125, 0.0).astype(BF16)
    for k in range(4):
        region = jnp.int32(-1)
        for s in range(slots):
            region = jnp.where(chosen[s][k], owner[1, s], region)
        send1[k, 0:SUB, :] = jnp.full((SUB, 2 * LANES), 1.0, F32) * region.astype(F32)
    first = []
    for part, (f0, f1) in enumerate(chunks):
        size = (f1 - f0) * edge
        for s in range(slots):
            loads[part, s].wait()
            rows = slice(s * frows + f0 * fine_edge, s * frows + f1 * fine_edge)
            high, low = split(fine[rows, :])
            got = jnp.dot(high, table, preferred_element_type=F32) + jnp.dot(
                low, table, preferred_element_type=F32
            )
            half_a[rows, :] = got[:, :LANES]
            half_b[rows, :] = got[:, LANES:]
        for h, half in enumerate((half_a, half_b)):
            averaged = []
            for s in range(slots):
                at = s * frows + f0 * fine_edge
                averaged.append(
                    half[pl.ds(at, size, stride=2), :] + half[pl.ds(at + 1, size, stride=2), :]
                )
            for k in range(4):
                total = averaged[0] * weight[0][k]
                for s in range(1, slots):
                    total = total + averaged[s] * weight[s][k]
                at = SUB + f0 * edge
                send1[k, at:at + size, h * LANES:(h + 1) * LANES] = total
        if part == 0:
            pl.semaphore_wait(barrier, len(peers))
        start = 0 if part == 0 else SUB + f0 * edge
        rows = pl.ds(start, SUB + f1 * edge - start)
        for k, delta in enumerate(DELTAS):
            copy = pltpu.make_async_remote_copy(
                src_ref=send1.at[k, rows], dst_ref=recv1.at[k, rows],
                send_sem=s1.at[part * 4 + k], recv_sem=r1.at[part * 4 + k],
                device_id=shifted(delta), device_id_type=MESH_ID,
            )
            copy.start()
            first.append(copy)

    for pair in range(4):
        row = iota((LANES, 2 * LANES), 0)
        col = iota((LANES, 2 * LANES), 1)
        hit = (row // edge == 2 * pair + col // LANES) & (row % edge == col % edge)
        place_table[pair] = both(jnp.where(hit, 1.0, 0.0).astype(BF16))
    planes[...] = jnp.zeros_like(planes)
    zrows[...] = jnp.zeros_like(zrows)
    corner_out[...] = jnp.zeros_like(corner_out)
    for k in range(4):
        send3[k * rows3 + e_at:k * rows3 + rows3, :] = jnp.zeros((edge, LANES), F32)
    coarse_load.wait()

    group = (iota((1, LANES), 1) // edge).astype(F32)
    second = []
    for part, (f0, f1) in enumerate(chunks):
        size = (f1 - f0) * edge
        for k in range(4):
            first[part * 4 + k].wait_recv()
        if part == 0:
            region_rows = [recv1[k, 0:1, 0:LANES] for k in range(4)]
            here = [group == region_rows[k] for k in range(4)]
        at = SUB + f0 * edge
        for h in range(2):
            stacked = split_lanes(jnp.concatenate(
                [recv1[k, at:at + size, h * LANES:(h + 1) * LANES] for k in range(4)], axis=0
            ))
            for pair in range(4):
                spread = jnp.dot(stacked, place_table[pair], preferred_element_type=F32)
                for odd in range(2):
                    y = h * SUB + 2 * pair + odd
                    rows = pl.ds(f0 * edge * edge + y, size, stride=edge)
                    merged = coarse[rows, :]
                    for k in range(4):
                        merged = jnp.where(
                            here[k], spread[k * size:(k + 1) * size, odd * LANES:(odd + 1) * LANES], merged
                        )
                    updated[rows, :] = merged
                    if y < 2:
                        halo_out[2, y, f0 * edge:f1 * edge, :] = merged
                    if y >= edge - 2:
                        halo_out[3, edge - 1 - y, f0 * edge:f1 * edge, :] = merged
        for f in range(f0, f1):
            for layer in range(2):
                for side, x in ((0, layer), (1, edge - 1 - layer)):
                    at = f * edge * edge + x * edge
                    halo_out[side, layer, f * edge:(f + 1) * edge, :] = updated[at:at + edge, :]
            for cx in (0, 1):
                for cy in (0, 1):
                    at = f * edge * edge + cx * (edge - 1) * edge + cy * (edge - 1)
                    corner_out[2 * cx + cy, f:f + 1, :] = updated[at:at + 1, :]
        rows = pl.ds(f0 * edge, size)
        for side in (2, 3, 0, 1):
            copy = pltpu.make_async_remote_copy(
                src_ref=halo_out.at[side, :, rows], dst_ref=halo_in.at[side ^ 1, :, rows],
                send_sem=s2.at[part * 4 + side], recv_sem=r2.at[part * 4 + (side ^ 1)],
                device_id=sides[side], device_id_type=MESH_ID,
            )
            copy.start()
            second.append(copy)
    for corner in range(4):
        copy = pltpu.make_async_remote_copy(
            src_ref=corner_out.at[corner], dst_ref=corner_in.at[3 - corner],
            send_sem=s2.at[8 + corner], recv_sem=r2.at[8 + 3 - corner],
            device_id=corners[corner], device_id_type=MESH_ID,
        )
        copy.start()
        second.append(copy)

    lane = iota((1, LANES), 1).astype(F32)

    def pick(k, place):
        t = lane - edge * region_rows[k] - place
        return jnp.where((t == 0.0) | (t == LANES) | (t == -LANES), 1.0, 0.0)

    i_side = iota((ext, 1), 0)
    place = jnp.where(i_side == edge, -1, jnp.where(i_side == edge + 1, edge, i_side)).astype(F32)
    used = i_side < edge + 2
    side_table = jnp.concatenate(
        [jnp.where(used, pick(k, place), 0.0) for k in range(4)], axis=0
    ).astype(BF16)
    side_table = jnp.concatenate([side_table, side_table], axis=1)
    i_z = iota((SUB, 1), 0)
    plus = jnp.where(i_z == 0, -1, jnp.where(i_z == 2, 0, jnp.where(i_z == 1, edge, edge + 1)))
    minus = jnp.where(i_z == 2, -2, edge - 1)
    z_list = []
    for k in range(4):
        up = pick(k, plus.astype(F32))
        down = jnp.where((i_z == 2) | (i_z == 3), pick(k, minus.astype(F32)), 0.0)
        z_list.append(jnp.where(i_z < 4, up - down, 0.0))
    z_table = jnp.concatenate(z_list, axis=0).astype(BF16)
    z_table = jnp.concatenate([z_table, z_table], axis=1)

    def z_store(v, values):
        for k in range(4):
            at = k * rows3
            level = values[k * SUB:k * SUB + 2, :]
            if v < edge:
                send3[pl.ds(at + z_at + v, 2, stride=edge), :] = level
                send3[pl.ds(at + zd_at + v, 2, stride=edge), :] = values[k * SUB + 2:k * SUB + 4, :]
            else:
                send3[pl.ds(at + e_at + 8 + v - edge, 2, stride=2), :] = level

    for v in range(edge):
        for f in range(fields):
            zrows[pl.ds(v * LANES + f, edge, stride=SUB), :] = updated[
                pl.ds(f * edge * edge + v, edge, stride=edge), :
            ]
    for v in range(0, edge, 2):
        got = times_transposed(z_table, split_lanes(zrows[v * LANES:(v + 2) * LANES, :]))
        z_store(v, got[:, :LANES])
        z_store(v + 1, got[:, LANES:])

    for copy in second:
        copy.wait_recv()

    for side in range(4):
        near = 1.0 if side % 2 == 0 else -1.0
        for f in range(fields):
            a = f * edge
            adjacent = halo_in[side, 0, a:a + edge, :]
            far = halo_in[side, 1, a:a + edge, :]
            own = halo_out[side, 0, a:a + edge, :]
            planes[pl.ds(2 * side * LANES + f, edge, stride=SUB), :] = adjacent
            planes[pl.ds((2 * side + 1) * LANES + f, edge, stride=SUB), :] = (own - far) * near
    for corner in range(4):
        planes[8 * LANES + corner * SUB:8 * LANES + (corner + 1) * SUB, :] = corner_in[corner]
    for side in range(4):
        both_planes = split_lanes(planes[2 * side * LANES:(2 * side + 2) * LANES, :])
        got = times_transposed(side_table, both_planes)
        for k in range(4):
            at = k * rows3
            send3[at + side * edge:at + (side + 1) * edge, :] = got[k * ext:k * ext + edge, :LANES]
            send3[at + e_at + 2 * side:at + e_at + 2 * side + 2, :] = (
                got[k * ext + edge:k * ext + edge + 2, :LANES]
            )
            to = at + d_at + side * edge
            send3[to:to + edge, :] = got[k * ext:k * ext + edge, LANES:]
        if side >= 2:
            z_store(edge + side - 2, times_transposed(z_table, both_planes[:LANES, :]))
    got = times_transposed(side_table, split_lanes(planes[8 * LANES:9 * LANES, :]))
    for k in range(4):
        send3[k * rows3 + c_at:k * rows3 + c_at + edge, :] = got[k * ext:k * ext + edge, :]

    third = []
    for k, delta in enumerate(DELTAS):
        copy = pltpu.make_async_remote_copy(
            src_ref=send3.at[pl.ds(k * rows3, rows3)], dst_ref=recv3.at[k],
            send_sem=s3.at[k], recv_sem=r3.at[k],
            device_id=shifted(-delta), device_id_type=MESH_ID,
        )
        copy.start()
        third.append(copy)
    for copy in third:
        copy.wait_recv()

    for s in range(slots):
        total = recv3[0] * weight[s][0]
        for k in range(1, 4):
            total = total + recv3[k] * weight[s][k]
        window[s] = total

    for copy in first + second + third:
        copy.wait_send()


def ghost_kernel(
    slots, fields, edge, count, mask, window, updated_in, updated_out, ghost_out,
    passing, ghost, pass_sem, out_sem,
):
    fine_edge = 2 * edge
    rows3, z_at, d_at, zd_at, c_at, e_at = window_rows(edge)
    live_count = count[0]
    into = pltpu.make_async_copy(updated_in, passing, pass_sem.at[0])
    into.start()

    def line_tables(cell, odd, pair):
        i = iota((2 * edge, LANES), 0)
        at = jnp.where(i == edge + pair, -1, jnp.where(i == edge + pair + 1, edge, i))
        at = jnp.where((i < edge) | (at != i), at, -9)
        plain = jnp.where(at == cell, 1.0, 0.0)
        sign = jnp.where(odd, 0.125, -0.125)
        slope = jnp.where(at == cell + 1, sign, jnp.where(at == cell - 1, -sign, 0.0))
        full = both(jnp.concatenate([plain, plain + slope], axis=1)).astype(BF16)
        return full, both((plain[:edge] * 0.125)).astype(BF16)

    l2 = iota((2 * edge, LANES), 1)
    side_tables = []
    for side in range(4):
        full, w_diff = line_tables((l2 % fine_edge) // 2, l2 % 2 == 1, 2 * side)
        side_tables.append(full)
    z_tables = []
    for z in range(2):
        full, v_diff = line_tables(
            (l2 % (2 * fine_edge)) // 4, (l2 // 2) % 2 == 1, 8 + 2 * z
        )
        z_tables.append(full)
    row = iota((LANES, LANES), 0)
    col = iota((LANES, LANES), 1)
    line_v = both(jnp.where(row // SUB == (col % (2 * fine_edge)) // 4, 1.0, 0.0).astype(BF16))

    lanes8 = iota((SUB, LANES), 1)
    low_half = lanes8 < 2 * fine_edge
    half_sign = jnp.where(low_half, -0.125, 0.125)
    quarter = (lanes8 // fine_edge) % 2 == 1
    quarter_slope = jnp.where(quarter, 0.125, -0.125)
    quarter_sign = jnp.where(quarter, 1.0, -1.0)
    last_sign = jnp.where(lanes8 % 2 == 1, 1.0, -1.0)
    own_field = lanes8 % SUB == iota((SUB, LANES), 0)

    def spread_plane(s, at, table, ends=None):
        total = window[s, at:at + edge, :]
        if ends is not None:
            total = jnp.concatenate([total, ends], axis=0)
        high = total.astype(BF16).astype(F32)
        tall = jnp.concatenate([high, total - high], axis=0)
        return jnp.dot(tall.T.astype(BF16), table, preferred_element_type=F32)

    def cut(values, m):
        return values[m * SUB:(m + 1) * SUB, :]

    outs = []
    for s in range(slots):
        keep = [
            jnp.where((s < live_count) & (mask[s, face] > 0), 1.0, 0.0).astype(F32)
            for face in range(6)
        ]
        ends_all = window[s, e_at:e_at + edge, :]
        lines = spread_plane(s, c_at, w_diff)
        line = [cut(lines, corner) * 8.0 for corner in range(4)]
        edges = []
        for side in range(4):
            centre = spread_plane(s, side * edge, side_tables[side], ends_all)
            diff = spread_plane(s, d_at + side * edge, w_diff)
            plain = [cut(centre, m)[:, :LANES] for m in range(edge)]
            full = [cut(centre, m)[:, LANES:] for m in range(edge)]
            high_side = side % 2
            if side < 2:
                edges.append(ends_all[2 * side:2 * side + 1, :])
                edges.append(ends_all[2 * side + 1:2 * side + 2, :])
                around = [line[2 * high_side]] + plain + [line[2 * high_side + 1]]
                for t in range(edge // 2):
                    base = jnp.where(low_half, full[2 * t], full[2 * t + 1])
                    slope = jnp.where(
                        low_half, around[2 * t + 2] - around[2 * t], around[2 * t + 3] - around[2 * t + 1]
                    )
                    across = jnp.where(low_half, cut(diff, 2 * t), cut(diff, 2 * t + 1))
                    base = base + slope * quarter_slope
                    at = t * LANES
                    ghost[s, :, side, at:at + LANES] = ((base - across) * keep[side])[:fields]
                    at = at + fine_edge * fine_edge
                    ghost[s, :, side, at:at + LANES] = ((base + across) * keep[side])[:fields]
            else:
                around = [line[high_side]] + plain + [line[2 + high_side]]
                for t in range(edge):
                    value = (
                        full[t] + (around[t + 2] - around[t]) * half_sign + cut(diff, t) * quarter_sign
                    )
                    ghost[s, :, side, t * LANES:(t + 1) * LANES] = (value * keep[side])[:fields]
        tall = jnp.concatenate([jnp.where(own_field, e, 0.0) for e in edges], axis=0)
        ends = jnp.dot(split_lanes(tall), line_v, preferred_element_type=F32)
        for z in range(2):
            centre = spread_plane(s, z_at + z * edge, z_tables[z], ends_all)
            diff = spread_plane(s, zd_at + z * edge, v_diff)
            around = (
                [cut(ends, z)] + [cut(centre, m)[:, :LANES] for m in range(edge)] + [cut(ends, 2 + z)]
            )
            for t in range(edge):
                value = (
                    cut(centre, t)[:, LANES:]
                    + (around[t + 2] - around[t]) * half_sign
                    + cut(diff, t) * last_sign
                )
                ghost[s, :, 4 + z, t * LANES:(t + 1) * LANES] = (value * keep[4 + z])[:fields]
        outs.append(pltpu.make_async_copy(ghost.at[s], ghost_out.at[s], out_sem.at[s]))
        outs[-1].start()
        if s == 0:
            into.wait()
            outs.append(pltpu.make_async_copy(passing, updated_out, pass_sem.at[1]))
            outs[-1].start()
    for copy in outs:
        copy.wait()


def body(n_box, n_lev, fine, coarse, owner_map, patch_count, face_mask):
    slots, fields, fine_edge, _ = fine.shape
    edge = fine_edge // 2
    block = fields * edge
    rows3 = window_rows(edge)[0]
    vmem = pl.BlockSpec(memory_space=pltpu.VMEM)
    smem = pl.BlockSpec(memory_space=pltpu.SMEM)
    far = pl.BlockSpec(memory_space=pl.ANY)
    flat = jax.ShapeDtypeStruct((block * edge, LANES), F32)
    updated, window = pl.pallas_call(
        functools.partial(kernel, n_box, n_lev, slots, fields, edge),
        out_shape=(flat, jax.ShapeDtypeStruct((slots, rows3, LANES), F32)),
        in_specs=[smem, smem, far, far],
        out_specs=(vmem, vmem),
        scratch_shapes=[
            pltpu.VMEM((slots * fields * fine_edge, fine_edge * fine_edge), F32),
            pltpu.VMEM((block * edge, LANES), F32),
            pltpu.VMEM((slots * fields * fine_edge, LANES), F32),
            pltpu.VMEM((slots * fields * fine_edge, LANES), F32),
            pltpu.VMEM((4, block + SUB, 2 * LANES), F32),
            pltpu.VMEM((4, block + SUB, 2 * LANES), F32),
            pltpu.VMEM((4, 2, block, LANES), F32),
            pltpu.VMEM((4, 2, block, LANES), F32),
            pltpu.VMEM((4, SUB, LANES), F32),
            pltpu.VMEM((4, SUB, LANES), F32),
            pltpu.VMEM((9 * LANES, LANES), F32),
            pltpu.VMEM((edge * LANES, LANES), F32),
            pltpu.VMEM((4 * rows3, LANES), F32),
            pltpu.VMEM((4, rows3, LANES), F32),
            pltpu.VMEM((4, 2 * LANES, 2 * LANES), BF16),
            pltpu.SemaphoreType.DMA((2 * slots + 1,)),
            pltpu.SemaphoreType.DMA((8,)),
            pltpu.SemaphoreType.DMA((8,)),
            pltpu.SemaphoreType.DMA((12,)),
            pltpu.SemaphoreType.DMA((12,)),
            pltpu.SemaphoreType.DMA((4,)),
            pltpu.SemaphoreType.DMA((4,)),
        ],
        compiler_params=pltpu.CompilerParams(collective_id=0, has_side_effects=True),
    )(
        owner_map.T, patch_count,
        fine.reshape(slots * fields * fine_edge, fine_edge * fine_edge),
        coarse.reshape(block * edge, LANES),
    )
    ghost_shape = (slots, fields, 6, 2 * fine_edge * fine_edge)
    updated, ghost = pl.pallas_call(
        functools.partial(ghost_kernel, slots, fields, edge),
        out_shape=(flat, jax.ShapeDtypeStruct(ghost_shape, F32)),
        in_specs=[smem, smem, vmem, far],
        out_specs=(far, far),
        scratch_shapes=[
            pltpu.VMEM((block * edge, LANES), F32),
            pltpu.VMEM(ghost_shape, F32),
            pltpu.SemaphoreType.DMA((2,)),
            pltpu.SemaphoreType.DMA((slots,)),
        ],
    )(patch_count, face_mask, window, updated)
    return updated.reshape(coarse.shape), ghost.transpose(0, 2, 1, 3)


def solution(mesh):
    return jax.shard_map(
        functools.partial(body, mesh.shape["box"], mesh.shape["lev"]),
        mesh=mesh,
        in_specs=(
            P(("box", "lev"), None, None, None),
            P(None, "box", "lev", None),
            P(("box", "lev"), None),
            P(("box", "lev")),
            P(("box", "lev"), None),
        ),
        out_specs=(P(None, "box", "lev", None), P(("box", "lev"), None, None, None)),
        check_vma=False,
    )
```

time: 35.7 us -> 31.4 us (0.88)
  local copies, waits for them, and re-layouts: 4.89 us -> 0 us
  Pallas kernels: 29.3 us -> 29.8 us
    unnamed x5 -> x0, local copies, waits for them, and re-layouts: 4.89 us -> none
    pallas_call x0 -> x1, Pallas kernels: none -> 3.6 us  [body(): pl.pallas_call(functools.partial(ghost_kernel, slots, fields, edge), out_...]
    pallas_call x1, Pallas kernels: 29.3 us -> 26.2 us  [body(): pl.pallas_call(functools.partial(kernel, n_box, n_lev, slots, fields, edg...]
where the time goes in v1:
time: 31.4 us; the launch traced here: 31.1 us
  Pallas kernels  29.8 us (95%)
  between operations  1.29 us (4%)
    pallas_call x1, Pallas kernels, body(): pl.pallas_call(functools.partial(kernel, n_box, n_lev, slots, fields, edg...  26.2 us
    pallas_call x1, Pallas kernels, body(): pl.pallas_call(functools.partial(ghost_kernel, slots, fields, edge), out_...  3.6 us

profile of v1, /device:TPU:0, one launch (start us, length us, event | category | flops | bytes accessed | tf_op | source)
XLA Modules:
  0.0 31.1 jit_solution(11122538002199789630)
XLA Ops:
  1.3 26.2 %shard_map.68 = (f32[1280,128]{1,0:T(8,128)}, f32[3,224,128]{2,1,0:T(8,128)}) custom-call(s32[2,3]{1,0:T(2,128)} %bitcast.7, s32[1]{0:T(128)S(6)} %copy.7.count, f32[480,1024]{1,0:T(8,128)} %bitcast.5, f32[1280,128]{1,0:T(8,128)} %bitcast.6), custom_call_target="tpu_custom_call" | custom-call | tf_op jit(solution)/shard_map/pallas_call | solution.py:433
  27.5 3.6 %shard_map.69 = (f32[1280,128]{1,0:T(8,128)}, f32[3,5,6,2048]{3,2,1,0:T(8,128)}) custom-call(s32[1]{0:T(128)S(6)} %copy.7.count, s32[3,6]{1,0:T(4,128)} %mask.1, f32[3,224,128]{2,1,0:T(8,128)} %get-tuple-element.6.window, f32[1280,128]{1,0:T(8,128)} %get-tuple-element.7.updated_in), custom_call_target="tpu_custom_call" | custom-call | tf_op jit(solution)/shard_map/pallas_call | solution.py:469

commit v2 on v1

--- a/solution.py
+++ b/solution.py
@@ -37,9 +37,7 @@
 
 
 def window_rows(edge):
-    z_at = 4 * edge
-    d_at = 6 * edge
-    return 14 * edge, z_at, d_at, d_at + 4 * edge, d_at + 6 * edge, d_at + 7 * edge
+    return 14 * edge, 0, 8 * edge, 2 * edge, 12 * edge, 13 * edge
 
 
 def kernel(
@@ -250,6 +248,20 @@
         z_store(v, got[:, :LANES])
         z_store(v + 1, got[:, LANES:])
 
+    third = []
+
+    def send_back(part):
+        start, size = ((0, 4 * edge), (4 * edge, rows3 - 4 * edge))[part]
+        for k, delta in enumerate(DELTAS):
+            copy = pltpu.make_async_remote_copy(
+                src_ref=send3.at[pl.ds(k * rows3 + start, size)], dst_ref=recv3.at[k, pl.ds(start, size)],
+                send_sem=s3.at[part * 4 + k], recv_sem=r3.at[part * 4 + k],
+                device_id=shifted(-delta), device_id_type=MESH_ID,
+            )
+            copy.start()
+            third.append(copy)
+
+    send_back(0)
     for copy in second:
         copy.wait_recv()
 
@@ -269,7 +281,7 @@
         got = times_transposed(side_table, both_planes)
         for k in range(4):
             at = k * rows3
-            send3[at + side * edge:at + (side + 1) * edge, :] = got[k * ext:k * ext + edge, :LANES]
+            send3[at + (4 + side) * edge:at + (5 + side) * edge, :] = got[k * ext:k * ext + edge, :LANES]
             send3[at + e_at + 2 * side:at + e_at + 2 * side + 2, :] = (
                 got[k * ext + edge:k * ext + edge + 2, :LANES]
             )
@@ -281,15 +293,7 @@
     for k in range(4):
         send3[k * rows3 + c_at:k * rows3 + c_at + edge, :] = got[k * ext:k * ext + edge, :]
 
-    third = []
-    for k, delta in enumerate(DELTAS):
-        copy = pltpu.make_async_remote_copy(
-            src_ref=send3.at[pl.ds(k * rows3, rows3)], dst_ref=recv3.at[k],
-            send_sem=s3.at[k], recv_sem=r3.at[k],
-            device_id=shifted(-delta), device_id_type=MESH_ID,
-        )
-        copy.start()
-        third.append(copy)
+    send_back(1)
     for copy in third:
         copy.wait_recv()
 
@@ -369,7 +373,7 @@
         line = [cut(lines, corner) * 8.0 for corner in range(4)]
         edges = []
         for side in range(4):
-            centre = spread_plane(s, side * edge, side_tables[side], ends_all)
+            centre = spread_plane(s, (4 + side) * edge, side_tables[side], ends_all)
             diff = spread_plane(s, d_at + side * edge, w_diff)
             plain = [cut(centre, m)[:, :LANES] for m in range(edge)]
             full = [cut(centre, m)[:, LANES:] for m in range(edge)]
@@ -456,8 +460,8 @@
             pltpu.SemaphoreType.DMA((8,)),
             pltpu.SemaphoreType.DMA((12,)),
             pltpu.SemaphoreType.DMA((12,)),
-            pltpu.SemaphoreType.DMA((4,)),
-            pltpu.SemaphoreType.DMA((4,)),
+            pltpu.SemaphoreType.DMA((8,)),
+            pltpu.SemaphoreType.DMA((8,)),
         ],
         compiler_params=pltpu.CompilerParams(collective_id=0, has_side_effects=True),
     )(

time: 31.4 us -> 31.3 us (level)
  no operation moved by 1% of the time
where the time goes in v2:
time: 31.3 us; the launch traced here: 31 us
  Pallas kernels  29.8 us (95%)
  between operations  1.29 us (4%)
    pallas_call x1, Pallas kernels, body(): pl.pallas_call(functools.partial(kernel, n_box, n_lev, slots, fields, edg...  26.2 us
    pallas_call x1, Pallas kernels, body(): pl.pallas_call(functools.partial(ghost_kernel, slots, fields, edge), out_...  3.59 us

profile of v2, /device:TPU:0, one launch (start us, length us, event | category | flops | bytes accessed | tf_op | source)
XLA Modules:
  0.0 31.0 jit_solution(16410067914183349750)
XLA Ops:
  1.3 26.2 %shard_map.68 = (f32[1280,128]{1,0:T(8,128)}, f32[3,224,128]{2,1,0:T(8,128)}) custom-call(s32[2,3]{1,0:T(2,128)} %bitcast.7, s32[1]{0:T(128)S(6)} %copy.7.count, f32[480,1024]{1,0:T(8,128)} %bitcast.5, f32[1280,128]{1,0:T(8,128)} %bitcast.6), custom_call_target="tpu_custom_call" | custom-call | tf_op jit(solution)/shard_map/pallas_call | solution.py:437
  27.5 3.6 %shard_map.69 = (f32[1280,128]{1,0:T(8,128)}, f32[3,5,6,2048]{3,2,1,0:T(8,128)}) custom-call(s32[1]{0:T(128)S(6)} %copy.7.count, s32[3,6]{1,0:T(4,128)} %mask.1, f32[3,224,128]{2,1,0:T(8,128)} %get-tuple-element.6.window, f32[1280,128]{1,0:T(8,128)} %get-tuple-element.7.updated_in), custom_call_target="tpu_custom_call" | custom-call | tf_op jit(solution)/shard_map/pallas_call | solution.py:473
